TPU v7x, 32 devices: a whole 2x2x4 slice. The times are simulated.
32 devices in a mesh: dp: 8 (over y, x, core), tensor: 4 (over z).
Axes of the slice: x: 2, y: 2, z: 4, core: 2. Of those that a mesh axis runs over, the one named last changes fastest.
Arguments:
- layer_input: float32 [16, 512, 2048], P('dp', 'tensor'), may hold values from -6 to 6
- segments: int32 [16, 512], P('dp'), may hold values from 0 to 7, never falling along the last dimension, each value on 1 to 256 neighbouring positions
- gain_attn: bfloat16 [2048], P('dp'), may hold values from 0.5 to 1.5
- w_qkv: bfloat16 [2048, 4, 640], P('dp', 'tensor'), as said below
- w_out_t: bfloat16 [2048, 2048], P('dp', 'tensor'), may hold values from -0.75 to 0.75
- gain_mlp: bfloat16 [2048], P('dp'), may hold values from 0.5 to 1.5
- w_gate_up: bfloat16 [2048, 2, 5632], P('dp', None, 'tensor'), may hold values from -0.125 to 0.125
- w_down_t: bfloat16 [2048, 5632], P('dp', 'tensor'), may hold values from -0.078125 to 0.078125
- cotangent: float32 [16, 512, 2048], P('dp', 'tensor'), may hold values from -6 to 6
Outputs:
- output: float32 [16, 512, 2048], P('dp', 'tensor')
- input_grad: float32 [16, 512, 2048], P('dp', 'tensor')
- gain_attn_grad: float32 [2048], P('dp')
- qkv_grad: float32 [2048, 4, 640], P('dp', 'tensor')
- out_grad: float32 [2048, 2048], P('dp', 'tensor')
- gain_mlp_grad: float32 [2048], P('dp')
- gate_up_grad: float32 [2048, 2, 5632], P('dp', None, 'tensor')
- down_grad: float32 [2048, 5632], P('dp', 'tensor')
Inputs may be any that keep to these rules, and one draw needn't show every extreme that they name: `w_qkv`: for each key-value group the columns hold the queries of its 8 heads, then its key, then its value.
All inputs are finite; a program needn't handle non-finite values.
Results may differ from a plain program's by a relative error of at most 0.013.
Values may be sent and summed in bfloat16 or wider, within the bound.
A program may use at most 256 MiB of HBM per device.

v0:
```python
import math
import jax
import jax.numpy as jnp
from jax import lax
from jax.sharding import PartitionSpec as P

H = 32
KV = 4
HD = 64
NORM_EPS = 1e-05


def rope_tables(segment_row, head_size):
    row_count = segment_row.shape[0]
    earlier = jnp.sum((segment_row[None, :] < segment_row[:, None]).astype(jnp.int32), axis=1)
    position = (jnp.arange(row_count, dtype=jnp.int32) - earlier).astype(jnp.float32)
    half_size = head_size // 2
    frequency = jnp.exp(
        jnp.arange(half_size, dtype=jnp.float32) * (-2.0 * math.log(10000.0) / head_size)
    )
    angles = position[:, None] * frequency[None, :]
    return (jnp.cos(angles), jnp.sin(angles))


def expand_table(angle_table, rank_count):
    return angle_table.reshape(
        (angle_table.shape[0],) + (1,) * (rank_count - 2) + (angle_table.shape[1],)
    )


def rotate(values, cosine, sine_tab):
    half_size = values.shape[-1] // 2
    cosine = expand_table(cosine, values.ndim)
    sine_tab = expand_table(sine_tab, values.ndim)
    first_half = values[..., :half_size]
    second_half = values[..., half_size:]
    return jnp.concatenate(
        [
            first_half * cosine - second_half * sine_tab,
            second_half * cosine + first_half * sine_tab,
        ],
        axis=-1,
    )


def unrotate(values, cosine, sine_tab):
    half_size = values.shape[-1] // 2
    cosine = expand_table(cosine, values.ndim)
    sine_tab = expand_table(sine_tab, values.ndim)
    first_half = values[..., :half_size]
    second_half = values[..., half_size:]
    return jnp.concatenate(
        [
            first_half * cosine + second_half * sine_tab,
            second_half * cosine - first_half * sine_tab,
        ],
        axis=-1,
    )


def allowed_pairs(segment_row):
    row_count = segment_row.shape[0]
    position = jnp.arange(row_count, dtype=jnp.int32)
    return (segment_row[:, None] == segment_row[None, :]) & (position[None, :] <= position[:, None])


def norm_forward(row_block, gain_row):
    inv_rms = lax.rsqrt(jnp.mean(row_block * row_block, axis=-1, keepdims=True) + NORM_EPS)
    return ((row_block * inv_rms * gain_row.astype(jnp.float32)).astype(jnp.bfloat16), inv_rms)


def norm_backward(row_block, inv_rms, gain_row, upstream):
    weighted = upstream * gain_row.astype(jnp.float32)
    back_term = inv_rms * weighted - row_block * (inv_rms * inv_rms * inv_rms) * jnp.mean(
        weighted * row_block, axis=-1, keepdims=True
    )
    return (back_term, jnp.sum(upstream * row_block * inv_rms, axis=0))


def split_heads(qkv_rows, head_group, head_size):
    row_count, groups = (qkv_rows.shape[0], qkv_rows.shape[1])
    query = qkv_rows[:, :, : head_group * head_size].reshape(
        row_count, groups, head_group, head_size
    )
    key_part = qkv_rows[:, :, head_group * head_size : (head_group + 1) * head_size]
    value_part = qkv_rows[:, :, (head_group + 1) * head_size :]
    return (query, key_part, value_part)


def score_block(query, key_part, allowed, head_size):
    scores = jnp.einsum("igne,jge->gnij", query, key_part, preferred_element_type=jnp.float32) * (
        1.0 / math.sqrt(head_size)
    )
    return jnp.where(allowed[None, None], scores, jnp.float32(-1e30))


def attend_forward(qkv_rows, segment_row, head_group, head_size):
    cosine, sine_tab = rope_tables(segment_row, head_size)
    query, key_part, value_part = split_heads(qkv_rows, head_group, head_size)
    query = rotate(query, cosine, sine_tab).astype(jnp.bfloat16)
    key_part = rotate(key_part, cosine, sine_tab).astype(jnp.bfloat16)
    value_part = value_part.astype(jnp.bfloat16)
    allowed = allowed_pairs(segment_row)
    scores = score_block(query, key_part, allowed, head_size)
    row_max = jnp.max(scores, axis=-1, keepdims=True)
    log_total = row_max + jnp.log(jnp.sum(jnp.exp(scores - row_max), axis=-1, keepdims=True))
    weights = jnp.exp(scores - log_total).astype(jnp.bfloat16)
    mixed = jnp.einsum("gnij,jge->igne", weights, value_part, preferred_element_type=jnp.float32)
    mixed = mixed.astype(jnp.bfloat16).reshape(qkv_rows.shape[0], -1)
    return (mixed, (query, key_part, value_part, log_total, cosine, sine_tab, allowed))


def attend_backward(grad_out, saved, head_size):
    query, key_part, value_part, log_total, cosine, sine_tab, allowed = saved
    row_count, groups, head_group = (query.shape[0], query.shape[1], query.shape[2])
    scores = score_block(query, key_part, allowed, head_size)
    weights = jnp.exp(scores - log_total)
    grad_heads = grad_out.reshape(row_count, groups, head_group, head_size)
    grad_value = jnp.einsum(
        "gnij,igne->jge",
        weights.astype(jnp.bfloat16),
        grad_heads,
        preferred_element_type=jnp.float32,
    )
    grad_weights = jnp.einsum(
        "igne,jge->gnij", grad_heads, value_part, preferred_element_type=jnp.float32
    )
    grad_scores = (
        weights
        * (grad_weights - jnp.sum(weights * grad_weights, axis=-1, keepdims=True))
        * (1.0 / math.sqrt(head_size))
    )
    grad_scores = grad_scores.astype(jnp.bfloat16)
    grad_query = jnp.einsum(
        "gnij,jge->igne", grad_scores, key_part, preferred_element_type=jnp.float32
    )
    grad_key = jnp.einsum("gnij,igne->jge", grad_scores, query, preferred_element_type=jnp.float32)
    grad_query = unrotate(grad_query, cosine, sine_tab).reshape(
        row_count, groups, head_group * head_size
    )
    grad_key = unrotate(grad_key, cosine, sine_tab)
    return jnp.concatenate([grad_query, grad_key, grad_value], axis=2).astype(jnp.bfloat16)


def outer_product(left_rows, right_rows):
    return lax.dot_general(
        left_rows, right_rows, (((0,), (0,)), ((), ())), preferred_element_type=jnp.float32
    )


def right_product(left_rows, right_matrix):
    return lax.dot_general(
        left_rows, right_matrix, (((1,), (1,)), ((), ())), preferred_element_type=jnp.float32
    )


def spread_forward(row_block):
    return lax.all_gather(row_block, "tensor", axis=0, tiled=True)


def spread_backward(row_block):
    return lax.all_gather(row_block, "tensor", axis=0, tiled=True)


def branch_sum(term_fn, local_rows):
    return lax.psum_scatter(
        term_fn(jnp.int32(0), lax.axis_size("tensor") * local_rows),
        "tensor",
        scatter_dimension=0,
        tiled=True,
    )


def input_sum(term_fn, local_rows):
    return lax.psum_scatter(
        term_fn(jnp.int32(0), lax.axis_size("tensor") * local_rows),
        "tensor",
        scatter_dimension=0,
        tiled=True,
    )


def add_terms(left_terms, right_terms):
    if left_terms is None:
        return right_terms
    return tuple((left_term + right_term for left_term, right_term in zip(left_terms, right_terms)))


def body(
    layer_input, segments, gain_attn, w_qkv, w_out_t, gain_mlp, w_gate_up, w_down_t, cotangent
):
    head_group = H // KV
    weight_shard = (gain_attn, w_qkv, w_out_t, gain_mlp, w_gate_up, w_down_t)
    local_rows = layer_input.shape[1]
    outputs = []
    input_grads = []
    grad_total = None
    owned_grads = None
    for number in range(layer_input.shape[0]):
        gathered_weights = (
            lax.all_gather(weight_shard[0], "dp", axis=0, tiled=True),
            lax.all_gather(weight_shard[1], "dp", axis=0, tiled=True),
            lax.all_gather(weight_shard[2], "dp", axis=0, tiled=True),
            lax.all_gather(weight_shard[3], "dp", axis=0, tiled=True),
            lax.all_gather(weight_shard[4], "dp", axis=0, tiled=True),
            lax.all_gather(weight_shard[5], "dp", axis=0, tiled=True),
        )
        g_attn, qkv_w, out_w, g_mlp, gu_w, down_w = gathered_weights
        model_width = qkv_w.shape[0]
        groups = qkv_w.shape[1]
        hidden_width = gu_w.shape[2]
        segment_row = segments[number]
        rows_in = layer_input[number]
        normed_attn, scale_attn = norm_forward(rows_in, g_attn)
        gathered_attn = spread_forward(normed_attn)
        row_count = gathered_attn.shape[0]
        qkv_rows = jnp.dot(
            gathered_attn, qkv_w.reshape(model_width, -1), preferred_element_type=jnp.float32
        ).reshape(row_count, groups, -1)
        mixed, saved = attend_forward(qkv_rows, segment_row, head_group, HD)

        def attn_term(row_start, row_span):
            return right_product(mixed, out_w)

        residual = rows_in + branch_sum(attn_term, local_rows)
        normed_mlp, scale_mlp = norm_forward(residual, g_mlp)
        gathered_mlp = spread_forward(normed_mlp)
        gate_up = jnp.dot(
            gathered_mlp, gu_w.reshape(model_width, -1), preferred_element_type=jnp.float32
        ).reshape(row_count, 2, hidden_width)
        gate_part = gate_up[:, 0]
        up_part = gate_up[:, 1]
        sigmoid_gate = jax.nn.sigmoid(gate_part)
        active = gate_part * sigmoid_gate
        hidden = (active * up_part).astype(jnp.bfloat16)

        def mlp_term(row_start, row_span):
            return right_product(hidden, down_w)

        outputs.append(residual + branch_sum(mlp_term, local_rows))
        back_weights = (
            lax.all_gather(weight_shard[0], "dp", axis=0, tiled=True),
            lax.all_gather(weight_shard[1], "dp", axis=0, tiled=True),
            lax.all_gather(weight_shard[2], "dp", axis=0, tiled=True),
            lax.all_gather(weight_shard[3], "dp", axis=0, tiled=True),
            lax.all_gather(weight_shard[4], "dp", axis=0, tiled=True),
            lax.all_gather(weight_shard[5], "dp", axis=0, tiled=True),
        )
        g_attn, qkv_w, out_w, g_mlp, gu_w, down_w = back_weights
        grad_in = cotangent[number]
        grad_rows = spread_backward(grad_in.astype(jnp.bfloat16))
        grad_down = outer_product(grad_rows, hidden)
        grad_hidden = jnp.dot(grad_rows, down_w, preferred_element_type=jnp.float32)
        grad_gu = jnp.stack(
            [
                grad_hidden * up_part * sigmoid_gate * (1.0 + gate_part * (1.0 - sigmoid_gate)),
                grad_hidden * active,
            ],
            axis=1,
        ).astype(jnp.bfloat16)
        flat_gu = grad_gu.reshape(row_count, -1)
        grad_gu_w = outer_product(gathered_mlp, flat_gu).reshape(model_width, 2, hidden_width)
        gu_flat = gu_w.reshape(model_width, -1)

        def mlp_back(row_start, row_span):
            return right_product(flat_gu, gu_flat)

        grad_normed_mlp = input_sum(mlp_back, local_rows)
        back_mlp, grad_g_mlp = norm_backward(residual, scale_mlp, g_mlp, grad_normed_mlp)
        grad_resid = grad_in + back_mlp
        resid_rows = spread_backward(grad_resid.astype(jnp.bfloat16))
        grad_out_w = outer_product(resid_rows, mixed)
        grad_mixed = jnp.dot(resid_rows, out_w, preferred_element_type=jnp.float32).astype(
            jnp.bfloat16
        )
        grad_qkv = attend_backward(grad_mixed, saved, HD)
        flat_qkv = grad_qkv.reshape(row_count, -1)
        grad_qkv_w = outer_product(gathered_attn, flat_qkv).reshape(qkv_w.shape)
        qkv_flat = qkv_w.reshape(model_width, -1)

        def attn_back(row_start, row_span):
            return right_product(flat_qkv, qkv_flat)

        grad_normed_attn = input_sum(attn_back, local_rows)
        back_attn, grad_g_attn = norm_backward(rows_in, scale_attn, g_attn, grad_normed_attn)
        input_grads.append(grad_resid + back_attn)
        grad_terms = (grad_g_attn, grad_qkv_w, grad_out_w, grad_g_mlp, grad_gu_w, grad_down)
        grad_total = add_terms(grad_total, grad_terms)
    owned_grads = lax.psum_scatter(grad_total, "dp", scatter_dimension=0, tiled=True)
    gain_first, gain_second = lax.psum((owned_grads[0], owned_grads[3]), "tensor")
    return (
        jnp.stack(outputs),
        jnp.stack(input_grads),
        gain_first,
        owned_grads[1],
        owned_grads[2],
        gain_second,
        owned_grads[4],
        owned_grads[5],
    )


def solution(mesh):
    placed = (
        P("dp", "tensor", None),
        P("dp", None),
        P("dp"),
        P("dp", "tensor", None),
        P("dp", "tensor"),
        P("dp"),
        P("dp", None, "tensor"),
        P("dp", "tensor"),
        P("dp", "tensor", None),
    )
    return jax.shard_map(
        body,
        mesh=mesh,
        in_specs=placed,
        out_specs=(
            P("dp", "tensor", None),
            P("dp", "tensor", None),
            P("dp"),
            P("dp", "tensor", None),
            P("dp", "tensor"),
            P("dp"),
            P("dp", None, "tensor"),
            P("dp", "tensor"),
        ),
        check_vma=False,
    )
```

profile of v0, /device:TPU:0, one launch (start us, length us, event | category | flops | bytes accessed | tf_op | source)
XLA Modules:
  0.0 1613.4 jit_solution(4839132049116461535)
XLA Ops:
  9.8 10.4 all-gather
  26.1 42.1 %all-gather.15.cloned.1.call-done = bf16[512,2048]{1,0:T(8,128)(2,1)} async-done(((bf16[128,2048]{1,0:T(8,128)(2,1)}), bf16[512,2048]{1,0:T(8,128)(2,1)}) %all-gather.15.cloned.1.call-update) | async-done | bytes 2097168 | tf_op jit(solution)/shard_map/all_gather | solution.py:158
  68.2 30.7 %all-gather.17.cloned.1.call-done = bf16[2048,1,640]{2,0,1:T(8,128)(2,1)} async-done(((bf16[256,1,640]{2,0,1:T(8,128)(2,1)}), bf16[2048,1,640]{2,0,1:T(8,128)(2,1)}) %all-gather.17.cloned.1.call-update) | async-done | bytes 2621456 | tf_op jit(solution)/shard_map/all_gather | solution.py:202
  98.9 4.2 fusion.37
  105.6 41.1 %all-gather.27.cloned.1.call-done = bf16[512,2048]{1,0:T(8,128)(2,1)} async-done(((bf16[128,2048]{1,0:T(8,128)(2,1)}), bf16[512,2048]{1,0:T(8,128)(2,1)}) %all-gather.27.cloned.1.call-update) | async-done | bytes 2097168 | tf_op jit(solution)/shard_map/all_gather | solution.py:158
  146.8 4.3 fusion.40
  151.1 3.0 fusion.116
  161.5 13.6 all-gather.19.cloned.1.call-done
  175.1 4.9 fusion.141
  192.3 3.4 convolution_convert_fusion.2
  195.8 3.3 fusion.143
  201.9 8.9 all-gather.1
  210.8 46.2 %reduce-scatter.13.cloned.1.call-done = f32[128,2048]{1,0:T(8,128)} async-done(((f32[512,2048]{1,0:T(8,128)}), f32[128,2048]{1,0:T(8,128)}) %reduce-scatter.13.cloned.1.call-update) | async-done | bytes 1048592 | tf_op jit(solution)/shard_map/reduce_scatter | solution.py:166
  257.0 79.5 %reduce-scatter.17.cloned.1.call-done = f32[128,2048]{1,0:T(8,128)} async-done(((f32[512,2048]{1,0:T(8,128)}), f32[128,2048]{1,0:T(8,128)}) %reduce-scatter.17.cloned.1.call-update) | async-done | bytes 1048592 | tf_op jit(solution)/shard_map/reduce_scatter | solution.py:166
  343.9 63.1 %all-gather.23.cloned.1.call-done = bf16[2048,2,1408]{2,0,1:T(8,128)(2,1)} async-done(((bf16[256,2,1408]{2,0,1:T(8,128)(2,1)}), bf16[2048,2,1408]{2,0,1:T(8,128)(2,1)}) %all-gather.23.cloned.1.call-update) | async-done | bytes 11534352 | tf_op jit(solution)/shard_map/all_gather | solution.py:205
  407.0 15.2 copy.87
  422.2 32.6 %all-gather.21.cloned.1.call-done = bf16[512,2048]{1,0:T(8,128)(2,1)} async-done(((bf16[128,2048]{1,0:T(8,128)(2,1)}), bf16[512,2048]{1,0:T(8,128)(2,1)}) %all-gather.21.cloned.1.call-update) | async-done | bytes 2097168 | tf_op jit(solution)/shard_map/all_gather | solution.py:158
  454.8 11.8 fusion.2
  466.6 34.8 %all-gather.31.cloned.1.call-done = bf16[512,2048]{1,0:T(8,128)(2,1)} async-done(((bf16[128,2048]{1,0:T(8,128)(2,1)}), bf16[512,2048]{1,0:T(8,128)(2,1)}) %all-gather.31.cloned.1.call-update) | async-done | bytes 2097168 | tf_op jit(solution)/shard_map/all_gather | solution.py:162
  501.5 43.8 %all-gather.25.cloned.1.call-done = bf16[2048,1408]{1,0:T(8,128)(2,1)} async-done(((bf16[256,1408]{1,0:T(8,128)(2,1)}), bf16[2048,1408]{1,0:T(8,128)(2,1)}) %all-gather.25.cloned.1.call-update) | async-done | bytes 5767184 | tf_op jit(solution)/shard_map/all_gather | solution.py:206
  545.2 9.0 multiply_bitcast_fusion.3
  555.8 10.3 convolution_bitcast_fusion.1
  566.2 76.9 %reduce-scatter.21.cloned.1.call-done = f32[128,2048]{1,0:T(8,128)} async-done(((f32[512,2048]{1,0:T(8,128)}), f32[128,2048]{1,0:T(8,128)}) %reduce-scatter.21.cloned.1.call-update) | async-done | bytes 1048592 | tf_op jit(solution)/shard_map/reduce_scatter | solution.py:175
  643.1 3.0 multiply_reduce_fusion.1
  647.0 45.4 %all-gather.29.cloned.1.call-done = bf16[512,2048]{1,0:T(8,128)(2,1)} async-done(((bf16[128,2048]{1,0:T(8,128)(2,1)}), bf16[512,2048]{1,0:T(8,128)(2,1)}) %all-gather.29.cloned.1.call-update) | async-done | bytes 2097168 | tf_op jit(solution)/shard_map/all_gather | solution.py:158
  692.4 11.8 fusion
  704.2 34.9 %all-gather.35.cloned.1.call-done = bf16[512,2048]{1,0:T(8,128)(2,1)} async-done(((bf16[128,2048]{1,0:T(8,128)(2,1)}), bf16[512,2048]{1,0:T(8,128)(2,1)}) %all-gather.35.cloned.1.call-update) | async-done | bytes 2097168 | tf_op jit(solution)/shard_map/all_gather | solution.py:162
  739.0 9.0 multiply_bitcast_fusion.1
  749.6 10.3 convolution_bitcast_fusion
  760.0 3.5 multiply_convert_fusion.1
  764.6 8.0 fusion.142
  773.0 3.6 multiply_convert_fusion
  777.7 7.7 fusion.144
  785.5 50.3 %reduce-scatter.25.cloned.1.call-done = f32[128,2048]{1,0:T(8,128)} async-done(((f32[512,2048]{1,0:T(8,128)}), f32[128,2048]{1,0:T(8,128)}) %reduce-scatter.25.cloned.1.call-update) | async-done | bytes 1048592 | tf_op jit(solution)/shard_map/reduce_scatter | solution.py:175
  837.3 78.0 %reduce-scatter.15.cloned.1.call-done = f32[128,2048]{1,0:T(8,128)} async-done(((f32[512,2048]{1,0:T(8,128)}), f32[128,2048]{1,0:T(8,128)}) %reduce-scatter.15.cloned.1.call-update) | async-done | bytes 1048592 | tf_op jit(solution)/shard_map/reduce_scatter | solution.py:166
  915.2 79.5 %reduce-scatter.19.cloned.1.call-done = f32[128,2048]{1,0:T(8,128)} async-done(((f32[512,2048]{1,0:T(8,128)}), f32[128,2048]{1,0:T(8,128)}) %reduce-scatter.19.cloned.1.call-update) | async-done | bytes 1048592 | tf_op jit(solution)/shard_map/reduce_scatter | solution.py:166
  994.7 5.3 fusion.138
  1000.7 5.4 fusion.146
  1006.1 6.1 add_bitcast_fusion
  1012.7 33.7 %all-gather.33.cloned.1.call-done = bf16[512,2048]{1,0:T(8,128)(2,1)} async-done(((bf16[128,2048]{1,0:T(8,128)(2,1)}), bf16[512,2048]{1,0:T(8,128)(2,1)}) %all-gather.33.cloned.1.call-update) | async-done | bytes 2097168 | tf_op jit(solution)/shard_map/all_gather | solution.py:162
  1046.4 2.9 convolution_convert_fusion.1
  1049.3 5.1 fusion.8
  1055.8 2.7 fusion.18
  1061.9 31.0 %all-gather.37.cloned.1.call-done = bf16[512,2048]{1,0:T(8,128)(2,1)} async-done(((bf16[128,2048]{1,0:T(8,128)(2,1)}), bf16[512,2048]{1,0:T(8,128)(2,1)}) %all-gather.37.cloned.1.call-update) | async-done | bytes 2097168 | tf_op jit(solution)/shard_map/all_gather | solution.py:162
  1092.9 2.9 convolution_convert_fusion
  1095.8 5.1 fusion.4
  1110.0 4.1 convolution_bitcast_fusion.3
  1114.5 3.3 convolution_bitcast_fusion.2
  1124.5 4.3 add_bitcast_fusion.1
  1128.9 5.6 fusion.25
  1134.8 5.5 fusion.27
  1145.3 13.4 fusion.21
  1161.7 17.7 %convolution_add_fusion = f32[2048,2,1408]{2,0,1:T(8,128)} fusion(f32[2048,2,1408]{2,0,1:T(8,128)} %fusion.21, bf16[512,2,1408]{0,2,1:T(8,128)(2,1)} %copy.110, bf16[512,2048]{1,0:T(8,128)(2,1)} %all-gather.29.cloned.1.call-done), kind=kOutput, calls=%fused_computation | convolution fusion | flops 5911347200 | bytes 51118080 | tf_op jit(solution)/shard_map/dot_general | solution.py:146
  1180.5 2.9 fusion.145
  1183.4 3.4 convolution_add_fusion.1
  1190.2 3.1 copy.114
  1193.3 48.5 %reduce-scatter.29.cloned.1.call-done = f32[256,1,640]{2,0,1:T(8,128)} async-done(((f32[2048,1,640]{2,0,1:T(8,128)}), f32[256,1,640]{2,0,1:T(8,128)}) %reduce-scatter.29.cloned.1.call-update) | async-done | bytes 655376 | tf_op jit(solution)/shard_map/reduce_scatter | solution.py:289
  1244.4 76.5 %reduce-scatter.27.cloned.1.call-done = f32[128,2048]{1,0:T(8,128)} async-done(((f32[512,2048]{1,0:T(8,128)}), f32[128,2048]{1,0:T(8,128)}) %reduce-scatter.27.cloned.1.call-update) | async-done | bytes 1048592 | tf_op jit(solution)/shard_map/reduce_scatter | solution.py:175
  1320.9 79.6 %reduce-scatter.23.cloned.1.call-done = f32[128,2048]{1,0:T(8,128)} async-done(((f32[512,2048]{1,0:T(8,128)}), f32[128,2048]{1,0:T(8,128)}) %reduce-scatter.23.cloned.1.call-update) | async-done | bytes 1048592 | tf_op jit(solution)/shard_map/reduce_scatter | solution.py:175
  1402.7 23.7 %all-reduce.2 = (f32[2048]{0:T(1024)S(1)}, f32[2048]{0:T(1024)S(1)}) all-reduce(f32[2048]{0:T(1024)S(1)} %add.202, f32[2048]{0:T(1024)S(1)} %add.206), channel_id=10, replica_groups=mesh['dp'=8,'tensor'=4] {'dp'}, use_global_device_ids=true, to_apply=%region_26.27.clone | all-reduce | flops 4096 | bytes 32768
  1426.5 12.0 all-reduce.3
  1442.4 108.7 %reduce-scatter.33.cloned.1.call-done = f32[256,2,1408]{2,0,1:T(8,128)} async-done(((f32[2048,2,1408]{2,0,1:T(8,128)}), f32[256,2,1408]{2,0,1:T(8,128)}) %reduce-scatter.33.cloned.1.call-update) | async-done | bytes 2883600 | tf_op jit(solution)/shard_map/reduce_scatter | solution.py:289
  1551.1 5.6 copy.113
  1556.7 49.4 %reduce-scatter.31.cloned.1.call-done = f32[256,512]{1,0:T(8,128)} async-done(((f32[2048,512]{1,0:T(8,128)}), f32[256,512]{1,0:T(8,128)}) %reduce-scatter.31.cloned.1.call-update) | async-done | bytes 524304 | tf_op jit(solution)/shard_map/reduce_scatter | solution.py:289
  (309 shorter events, 91.1 us)
Async XLA Ops:
  7.2 13.7 copy-start.2
  7.2 61.0 %all-gather.15.cloned.1.call-start = ((), (), s32[]{:S(2)}) async-start(), calls=%async_computation.12 | async-start | bytes 2621440 | tf_op jit(solution)/shard_map/all_gather | solution.py:158
  9.8 14.4 copy-start.81
  22.1 76.8 %all-gather.17.cloned.1.call-start = ((), (), s32[]{:S(2)}) async-start(), calls=%async_computation.13 | async-start | bytes 2949120 | tf_op jit(solution)/shard_map/all_gather | solution.py:202
  22.9 123.9 %all-gather.27.cloned.1.call-start = ((), (), s32[]{:S(2)}) async-start(), calls=%async_computation.20 | async-start | bytes 2621440 | tf_op jit(solution)/shard_map/all_gather | solution.py:158
  23.6 151.5 %all-gather.19.cloned.1.call-start = ((), (), s32[]{:S(2)}) async-start(), calls=%async_computation.14 | async-start | bytes 2359296 | tf_op jit(solution)/shard_map/all_gather | solution.py:203
  24.2 232.8 %reduce-scatter.13.cloned.1.call-start = ((), (), s32[]{:S(2)}) async-start(), calls=%async_computation.15 | async-start | bytes 5242880 | tf_op jit(solution)/shard_map/reduce_scatter | solution.py:166
  24.2 74.7 %copy-start.68 = (s32[1,512]{1,0:T(1,128)}, s32[1,512]{1,0:T(1,128)S(1)}, u32[]{:S(2)}) copy-start(s32[1,512]{1,0:T(1,128)S(1)} %get-tuple-element.90) | copy-start | bytes 6148
  24.8 126.2 %copy-start.70 = (f32[512]{0:T(512)}, f32[512]{0:T(512)S(1)}, u32[]{:S(2)}) copy-start(f32[512]{0:T(512)S(1)} %get-tuple-element.119) | copy-start | bytes 6148
  24.8 126.2 %copy-start.72 = (f32[512]{0:T(512)}, f32[512]{0:T(512)S(1)}, u32[]{:S(2)}) copy-start(f32[512]{0:T(512)S(1)} %get-tuple-element.120) | copy-start | bytes 6148
  24.9 126.2 %copy-start.79 = (f32[32]{0:T(128)}, f32[32]{0:T(128)S(1)}, u32[]{:S(2)}) copy-start(f32[32]{0:T(128)S(1)} %multiply_exponential_fusion) | copy-start | bytes 388
  105.6 48.5 %copy-start.14 = (f32[512,1,512]{0,2,1:T(8,128)S(1)}, f32[512,1,512]{0,2,1:T(8,128)}, u32[]{:S(2)}) copy-start(f32[512,1,512]{0,2,1:T(8,128)} %copy.82) | copy-start | bytes 3145732
  146.8 7.4 copy-start.56
  146.8 7.4 copy-start.58
  154.1 33.4 %copy-start.44 = (bf16[512,32]{1,0:T(8,128)(2,1)}, bf16[512,32]{1,0:T(8,128)(2,1)S(1)}, u32[]{:S(2)}) copy-start(bf16[512,32]{1,0:T(8,128)(2,1)S(1)} %get-tuple-element.105) | copy-start | bytes 98308
  161.5 18.5 %copy-start.20 = (bf16[64,8,512]{2,0,1:T(8,128)(2,1)}, bf16[64,8,512]{2,0,1:T(8,128)(2,1)S(1)}, u32[]{:S(2)}) copy-start(bf16[64,8,512]{2,0,1:T(8,128)(2,1)S(1)} %convolution_convert_fusion.3) | copy-start | bytes 1572868
  180.0 5.8 copy-start.52
  180.0 5.8 copy-start.54
  180.0 156.4 %reduce-scatter.17.cloned.1.call-start = ((), (), s32[]{:S(2)}) async-start(), calls=%async_computation.21 | async-start | bytes 5242880 | tf_op jit(solution)/shard_map/reduce_scatter | solution.py:166
  180.9 9.9 copy-start.11
  180.9 6.6 copy-start.46
  199.1 207.9 %all-gather.23.cloned.1.call-start = ((), (), s32[]{:S(2)}) async-start(), calls=%async_computation.17 | async-start | bytes 12976128 | tf_op jit(solution)/shard_map/all_gather | solution.py:205
  201.8 253.0 %all-gather.21.cloned.1.call-start = ((), (), s32[]{:S(2)}) async-start(), calls=%async_computation.16 | async-start | bytes 2621440 | tf_op jit(solution)/shard_map/all_gather | solution.py:158
  340.2 161.3 %all-gather.31.cloned.1.call-start = ((), (), s32[]{:S(2)}) async-start(), calls=%async_computation.24 | async-start | bytes 2621440 | tf_op jit(solution)/shard_map/all_gather | solution.py:162
  342.9 202.4 %all-gather.25.cloned.1.call-start = ((), (), s32[]{:S(2)}) async-start(), calls=%async_computation.18 | async-start | bytes 6488064 | tf_op jit(solution)/shard_map/all_gather | solution.py:206
  343.5 299.6 %reduce-scatter.21.cloned.1.call-start = ((), (), s32[]{:S(2)}) async-start(), calls=%async_computation.25 | async-start | bytes 5242880 | tf_op jit(solution)/shard_map/reduce_scatter | solution.py:175
  566.1 77.0 %copy-start.6 = (f32[128,2048]{1,0:T(8,128)S(1)}, f32[128,2048]{1,0:T(8,128)}, u32[]{:S(2)}) copy-start(f32[128,2048]{1,0:T(8,128)} %get-tuple-element.69) | copy-start | bytes 3145732
  566.1 126.3 %all-gather.29.cloned.1.call-start = ((), (), s32[]{:S(2)}) async-start(), calls=%async_computation.22 | async-start | bytes 2621440 | tf_op jit(solution)/shard_map/all_gather | solution.py:158
  646.1 93.0 %all-gather.35.cloned.1.call-start = ((), (), s32[]{:S(2)}) async-start(), calls=%async_computation.28 | async-start | bytes 2621440 | tf_op jit(solution)/shard_map/all_gather | solution.py:162
  646.8 188.9 %reduce-scatter.25.cloned.1.call-start = ((), (), s32[]{:S(2)}) async-start(), calls=%async_computation.29 | async-start | bytes 5242880 | tf_op jit(solution)/shard_map/reduce_scatter | solution.py:175
  760.0 155.2 %reduce-scatter.15.cloned.1.call-start = ((), (), s32[]{:S(2)}) async-start(), calls=%async_computation.19 | async-start | bytes 5242880 | tf_op jit(solution)/shard_map/reduce_scatter | solution.py:166
  772.7 222.0 %reduce-scatter.19.cloned.1.call-start = ((), (), s32[]{:S(2)}) async-start(), calls=%async_computation.23 | async-start | bytes 5242880 | tf_op jit(solution)/shard_map/reduce_scatter | solution.py:166
  785.4 209.3 %copy-start.15 = (f32[128,2048]{1,0:T(8,128)S(1)}, f32[128,2048]{1,0:T(8,128)}, u32[]{:S(2)}) copy-start(f32[128,2048]{1,0:T(8,128)} %reduce-scatter.21.cloned.1.call-done) | copy-start | bytes 3145732
  785.4 261.0 %all-gather.33.cloned.1.call-start = ((), (), s32[]{:S(2)}) async-start(), calls=%async_computation.26 | async-start | bytes 2621440 | tf_op jit(solution)/shard_map/all_gather | solution.py:162
  1000.1 92.8 %all-gather.37.cloned.1.call-start = ((), (), s32[]{:S(2)}) async-start(), calls=%async_computation.30 | async-start | bytes 2621440 | tf_op jit(solution)/shard_map/all_gather | solution.py:162
  1000.7 5.5 copy-start.8
  1000.7 189.6 %reduce-scatter.35.cloned.1.call-start = ((), (), s32[]{:S(2)}) async-start(), calls=%async_computation.35 | async-start | bytes 12976128 | tf_op jit(solution)/shard_map/reduce_scatter | solution.py:289
  1000.7 5.4 copy-start.35
  1012.2 34.2 %copy-start.10 = (bf16[2048,512]{1,0:T(8,128)(2,1)S(1)}, bf16[2048,512]{1,0:T(8,128)(2,1)}, u32[]{:S(2)}) copy-start(bf16[2048,512]{1,0:T(8,128)(2,1)} %all-gather.19.cloned.1.call-done) | copy-start | bytes 6291460
  1012.2 229.6 %reduce-scatter.29.cloned.1.call-start = ((), (), s32[]{:S(2)}) async-start(), calls=%async_computation.32 | async-start | bytes 5898240 | tf_op jit(solution)/shard_map/reduce_scatter | solution.py:289
  1049.3 5.1 copy-start.60
  1049.3 6.5 slice-start.1
  1061.9 33.9 %copy-start.12 = (pred[512,512]{0,1:T(8,128)(4,1)S(1)}, pred[512,512]{0,1:T(8,128)(4,1)}, u32[]{:S(2)}) copy-start(pred[512,512]{0,1:T(8,128)(4,1)} %copy-done.11) | copy-start | bytes 786436
  1061.9 33.9 %copy-start.65 = (f32[8,512]{1,0:T(8,128)S(1)}, f32[8,512]{1,0:T(8,128)}, u32[]{:S(2)}) copy-start(f32[8,512]{1,0:T(8,128)} %copy-done.64) | copy-start | bytes 49156
  1095.8 5.2 copy-start.62
  1095.8 5.2 slice-start.4
  1095.8 7.1 slice-start.5
  1110.0 7.8 copy-start.53
  1110.0 7.8 copy-start.55
  1110.0 8.0 slice-start.2
  1114.5 7.8 slice-start.6
  1128.9 192.0 %reduce-scatter.27.cloned.1.call-start = ((), (), s32[]{:S(2)}) async-start(), calls=%async_computation.31 | async-start | bytes 5242880 | tf_op jit(solution)/shard_map/reduce_scatter | solution.py:175
  1134.5 266.0 %reduce-scatter.23.cloned.1.call-start = ((), (), s32[]{:S(2)}) async-start(), calls=%async_computation.27 | async-start | bytes 5242880 | tf_op jit(solution)/shard_map/reduce_scatter | solution.py:175
  1140.4 410.7 %reduce-scatter.33.cloned.1.call-start = ((), (), s32[]{:S(2)}) async-start(), calls=%async_computation.34 | async-start | bytes 25952256 | tf_op jit(solution)/shard_map/reduce_scatter | solution.py:289
  1145.3 13.4 copy-start.41
  1145.3 13.4 copy-start.43
  1179.5 426.6 %reduce-scatter.31.cloned.1.call-start = ((), (), s32[]{:S(2)}) async-start(), calls=%async_computation.33 | async-start | bytes 4718592 | tf_op jit(solution)/shard_map/reduce_scatter | solution.py:289
  1190.2 210.4 %copy-start.3 = (f32[2,128,2048]{2,1,0:T(8,128)S(1)}, f32[2,128,2048]{2,1,0:T(8,128)}, u32[]{:S(2)}) copy-start(f32[2,128,2048]{2,1,0:T(8,128)} %param.9) | copy-start | bytes 6291460
  1190.2 210.4 %copy-start.67 = (f32[8,1,256]{2,1,0:T(1,128)S(1)}, f32[8,1,256]{2,1,0:T(1,128)}, u32[]{:S(2)}) copy-start(f32[8,1,256]{2,1,0:T(1,128)} %copy-done.66) | copy-start | bytes 24580
  1190.2 210.4 %copy-start.76 = (f32[128]{0:T(128)S(1)}, f32[128]{0:T(128)}, u32[]{:S(2)}) copy-start(f32[128]{0:T(128)} %copy-done.75) | copy-start | bytes 1540
  1190.2 210.4 %copy-start.78 = (f32[128]{0:T(128)S(1)}, f32[128]{0:T(128)}, u32[]{:S(2)}) copy-start(f32[128]{0:T(128)} %copy-done.77) | copy-start | bytes 1540
  1193.3 245.2 %copy-start.82 = (f32[128]{0:T(128)S(1)}, f32[128]{0:T(128)}, u32[]{:S(2)}) copy-start(f32[128]{0:T(128)} %get-tuple-element.97) | copy-start | bytes 1540
  1193.3 245.2 %copy-start.83 = (f32[128]{0:T(128)S(1)}, f32[128]{0:T(128)}, u32[]{:S(2)}) copy-start(f32[128]{0:T(128)} %get-tuple-element.118) | copy-start | bytes 1540
  1320.9 117.6 %copy-start.18 = (f32[128,2048]{1,0:T(8,128)S(1)}, f32[128,2048]{1,0:T(8,128)}, u32[]{:S(2)}) copy-start(f32[128,2048]{1,0:T(8,128)} %reduce-scatter.27.cloned.1.call-done) | copy-start | bytes 3145732
  (54 other events, 138.6 us)
Sparse Core Ops, SparseCore 0:
  22.2 45.9 all-gather.14
  70.1 28.7 all-gather.16
  101.1 45.6 all-gather.26
  148.5 26.5 all-gather.18
  180.1 76.7 reduce-scatter.12
  259.1 77.2 reduce-scatter.16
  338.9 68.0 all-gather.22
  409.2 45.6 all-gather.20
  457.0 44.4 all-gather.30
  503.2 41.9 all-gather.24
  566.3 76.7 reduce-scatter.20
  646.2 46.1 all-gather.28
  694.5 44.4 all-gather.34
  760.1 75.5 reduce-scatter.24
  837.9 77.2 reduce-scatter.14
  917.4 77.2 reduce-scatter.18
  1000.2 46.1 all-gather.32
  1048.4 44.4 all-gather.36
  1096.4 85.6 reduce-scatter.34
  1185.3 56.4 reduce-scatter.28
  1244.1 76.7 reduce-scatter.26
  1323.2 77.2 reduce-scatter.22
  1404.2 146.8 reduce-scatter.32
  1554.9 51.1 reduce-scatter.30
where the time goes:
time: 1620 us; the launch traced here: 1610 us
  waiting for transfers between devices  1220 us (75%)
  matrix products  200 us (12%)
  local copies, waits for them, and re-layouts  62.7 us (4%)
  blocking collectives  55 us (3%)
  other arithmetic  52.8 us (3%)
  between operations  16.8 us (1%)
    reduce_scatter x4, waiting for transfers between devices, input_sum(): lax.psum_scatter(term_fn(jnp.int32(0), lax.axis_size('tensor') * local_ro...  283 us
    reduce_scatter x4, waiting for transfers between devices, branch_sum(): lax.psum_scatter(term_fn(jnp.int32(0), lax.axis_size('tensor') * local_ro...  283 us
    reduce_scatter x4, waiting for transfers between devices, body(): lax.psum_scatter(grad_total, 'dp', scatter_dimension=0, tiled=True)  207 us
    all_gather x4, waiting for transfers between devices, spread_forward(): return lax.all_gather(row_block, 'tensor', axis=0, tiled=True)  161 us
    all_gather x4, waiting for transfers between devices, spread_backward(): return lax.all_gather(row_block, 'tensor', axis=0, tiled=True)  134 us
    all_gather x1, waiting for transfers between devices, body(): lax.all_gather(weight_shard[4], 'dp', axis=0, tiled=True)  63.1 us
    dot_general x8, matrix products, right_product(): lax.dot_general(left_rows, right_matrix, (((1,), (1,)), ((), ())), prefer...  55.7 us
    dot_general x8, matrix products, outer_product(): lax.dot_general(left_rows, right_rows, (((0,), (0,)), ((), ())), preferre...  55.1 us
  transfers between devices with their start and end apart: 24, of which 23 were waited for; matrix products, arithmetic and copies ran while one was open for 15% of the time, Pallas kernels for 0%

commit v1 on v0

--- a/solution.py
+++ b/solution.py
@@ -8,6 +8,13 @@
 KV = 4
 HD = 64
 NORM_EPS = 1e-05
+
+
+def swapped_in(array, name, d):
+    size = lax.axis_size(name)
+    tiles = jnp.stack([array for _ in range(size)])
+    tiles = lax.all_to_all(tiles, name, split_axis=0, concat_axis=0)
+    return jnp.concatenate(tiles, axis=d)
 
 
 def rope_tables(segment_row, head_size):
@@ -155,7 +162,7 @@
 
 
 def spread_forward(row_block):
-    return lax.all_gather(row_block, "tensor", axis=0, tiled=True)
+    return swapped_in(row_block, "tensor", 0)
 
 
 def spread_backward(row_block):

time: 1620 us -> 1550 us (0.957)
  waiting for transfers between devices: 1220 us -> 1080 us
  blocking collectives: 55 us -> 108 us
    all_gather x4 -> x0, waiting for transfers between devices: 161 us -> none  [spread_forward(): return lax.all_gather(row_block, 'tensor', axis=0, tiled=True)]
    all_to_all x0 -> x3, waiting for transfers between devices: none -> 120 us  [swapped_in(): tiles = lax.all_to_all(tiles, name, split_axis=0, concat_axis=0)]
    all_to_all x0 -> x1, blocking collectives: none -> 53.5 us  [swapped_in(): tiles = lax.all_to_all(tiles, name, split_axis=0, concat_axis=0)]
    all_gather x4, waiting for transfers between devices: 134 us -> 85.4 us  [spread_backward(): return lax.all_gather(row_block, 'tensor', axis=0, tiled=True)]
    all_gather x1, waiting for transfers between devices: 30.7 us -> 0.01 us  [body(): lax.all_gather(weight_shard[1], 'dp', axis=0, tiled=True)]
    unnamed x197 -> x189, local copies, waits for them, and re-layouts: 32.6 us -> 32.4 us
  transfers between devices with their start and end apart: 24 -> 23, of which waited for: 23 -> 18; matrix products, arithmetic and copies ran while one was open for 15% -> 16% of each run, Pallas kernels for 0% -> 0%
where the time goes in v1:
time: 1550 us; the launch traced here: 1540 us
  waiting for transfers between devices  1080 us (70%)
  matrix products  202 us (13%)
  blocking collectives  108 us (7%)
  local copies, waits for them, and re-layouts  64.6 us (4%)
  other arithmetic  50 us (3%)
  between operations  16.7 us (1%)
  starting transfers between devices  15.8 us (1%)
    reduce_scatter x4, waiting for transfers between devices, input_sum(): lax.psum_scatter(term_fn(jnp.int32(0), lax.axis_size('tensor') * local_ro...  283 us
    reduce_scatter x4, waiting for transfers between devices, branch_sum(): lax.psum_scatter(term_fn(jnp.int32(0), lax.axis_size('tensor') * local_ro...  282 us
    reduce_scatter x4, waiting for transfers between devices, body(): lax.psum_scatter(grad_total, 'dp', scatter_dimension=0, tiled=True)  204 us
    all_to_all x3, waiting for transfers between devices, swapped_in(): tiles = lax.all_to_all(tiles, name, split_axis=0, concat_axis=0)  120 us
    all_gather x4, waiting for transfers between devices, spread_backward(): return lax.all_gather(row_block, 'tensor', axis=0, tiled=True)  85.4 us
    all_gather x1, waiting for transfers between devices, body(): lax.all_gather(weight_shard[4], 'dp', axis=0, tiled=True)  61.3 us
    dot_general x8, matrix products, outer_product(): lax.dot_general(left_rows, right_rows, (((0,), (0,)), ((), ())), preferre...  56.3 us
    dot_general x8, matrix products, right_product(): lax.dot_general(left_rows, right_matrix, (((1,), (1,)), ((), ())), prefer...  55.8 us
  transfers between devices with their start and end apart: 23, of which 18 were waited for; matrix products, arithmetic and copies ran while one was open for 16% of the time, Pallas kernels for 0%

profile of v1, /device:TPU:0, one launch (start us, length us, event | category | flops | bytes accessed | tf_op | source)
XLA Modules:
  0.0 1539.9 jit_solution(15488686930300862107)
XLA Ops:
  10.3 10.4 all-gather
  22.1 53.5 %all_to_all.20 = bf16[4,128,2048]{2,1,0:T(8,128)(2,1)} all-to-all(bf16[4,128,2048]{2,1,0:T(8,128)(2,1)S(1)} %stack.73), channel_id=1, replica_groups=mesh['dp'=8,'tensor'=4] {'tensor'}, dimensions={0} | all-to-all | bytes 4194304 | tf_op jit(solution)/shard_map/all_to_all | solution.py:16
  77.2 4.5 all-to-all-start
  84.3 4.2 fusion.36
  91.1 38.5 %all-to-all-done = bf16[4,128,2048]{2,1,0:T(8,128)(2,1)} async-done(((bf16[4,128,2048]{2,1,0:T(8,128)(2,1)}), bf16[4,128,2048]{2,1,0:T(8,128)(2,1)}, u32[]{:S(2)}, u32[]{:S(2)}) %all-to-all-start) | async-done | bytes 2097184 | tf_op jit(solution)/shard_map/all_to_all | solution.py:16
  129.6 4.3 fusion.33
  133.9 3.0 fusion.110
  144.4 5.0 fusion.137
  161.5 3.3 fusion.135
  171.1 8.9 all-gather.1
  180.0 44.5 %reduce-scatter.17.cloned.1.call-done = f32[128,2048]{1,0:T(8,128)} async-done(((f32[512,2048]{1,0:T(8,128)}), f32[128,2048]{1,0:T(8,128)}) %reduce-scatter.17.cloned.1.call-update) | async-done | bytes 1048592 | tf_op jit(solution)/shard_map/reduce_scatter | solution.py:173
  224.5 79.5 %reduce-scatter.13.cloned.1.call-done = f32[128,2048]{1,0:T(8,128)} async-done(((f32[512,2048]{1,0:T(8,128)}), f32[128,2048]{1,0:T(8,128)}) %reduce-scatter.13.cloned.1.call-update) | async-done | bytes 1048592 | tf_op jit(solution)/shard_map/reduce_scatter | solution.py:173
  304.0 2.8 multiply_reduce_fusion.5
  308.5 4.2 all-to-all-start.1
  313.1 61.3 %all-gather.15.cloned.1.call-done = bf16[2048,2,1408]{2,0,1:T(8,128)(2,1)} async-done(((bf16[256,2,1408]{2,0,1:T(8,128)(2,1)}), bf16[2048,2,1408]{2,0,1:T(8,128)(2,1)}) %all-gather.15.cloned.1.call-update) | async-done | bytes 11534352 | tf_op jit(solution)/shard_map/all_gather | solution.py:212
  374.4 15.2 copy.87
  389.6 11.9 fusion.2
  401.5 20.6 %all-gather.19.cloned.1.call-done = bf16[512,2048]{1,0:T(8,128)(2,1)} async-done(((bf16[128,2048]{1,0:T(8,128)(2,1)}), bf16[512,2048]{1,0:T(8,128)(2,1)}) %all-gather.19.cloned.1.call-update) | async-done | bytes 2097168 | tf_op jit(solution)/shard_map/all_gather | solution.py:169
  422.1 43.9 %all-gather.17.cloned.1.call-done = bf16[2048,1408]{1,0:T(8,128)(2,1)} async-done(((bf16[256,1408]{1,0:T(8,128)(2,1)}), bf16[2048,1408]{1,0:T(8,128)(2,1)}) %all-gather.17.cloned.1.call-update) | async-done | bytes 5767184 | tf_op jit(solution)/shard_map/all_gather | solution.py:213
  466.0 9.0 multiply_bitcast_fusion.3
  476.6 10.4 convolution_bitcast_fusion.1
  487.0 76.9 %reduce-scatter.21.cloned.1.call-done = f32[128,2048]{1,0:T(8,128)} async-done(((f32[512,2048]{1,0:T(8,128)}), f32[128,2048]{1,0:T(8,128)}) %reduce-scatter.21.cloned.1.call-update) | async-done | bytes 1048592 | tf_op jit(solution)/shard_map/reduce_scatter | solution.py:182
  567.7 4.5 all-to-all-start.3
  573.2 81.5 %all-to-all-done.3 = bf16[4,128,2048]{2,1,0:T(8,128)(2,1)} async-done(((bf16[4,128,2048]{2,1,0:T(8,128)(2,1)}), bf16[4,128,2048]{2,1,0:T(8,128)(2,1)}, u32[]{:S(2)}, u32[]{:S(2)}) %all-to-all-start.3) | async-done | bytes 2097184 | tf_op jit(solution)/shard_map/all_to_all | solution.py:16
  654.7 11.8 fusion
  666.5 9.0 multiply_bitcast_fusion.1
  677.0 10.3 convolution_bitcast_fusion
  687.4 3.5 multiply_convert_fusion.1
  692.0 7.8 fusion.136
  700.1 3.6 multiply_convert_fusion
  704.8 7.7 fusion.138
  712.6 49.9 %reduce-scatter.25.cloned.1.call-done = f32[128,2048]{1,0:T(8,128)} async-done(((f32[512,2048]{1,0:T(8,128)}), f32[128,2048]{1,0:T(8,128)}) %reduce-scatter.25.cloned.1.call-update) | async-done | bytes 1048592 | tf_op jit(solution)/shard_map/reduce_scatter | solution.py:182
  764.0 78.1 %reduce-scatter.15.cloned.1.call-done = f32[128,2048]{1,0:T(8,128)} async-done(((f32[512,2048]{1,0:T(8,128)}), f32[128,2048]{1,0:T(8,128)}) %reduce-scatter.15.cloned.1.call-update) | async-done | bytes 1048592 | tf_op jit(solution)/shard_map/reduce_scatter | solution.py:173
  842.1 79.5 %reduce-scatter.19.cloned.1.call-done = f32[128,2048]{1,0:T(8,128)} async-done(((f32[512,2048]{1,0:T(8,128)}), f32[128,2048]{1,0:T(8,128)}) %reduce-scatter.19.cloned.1.call-update) | async-done | bytes 1048592 | tf_op jit(solution)/shard_map/reduce_scatter | solution.py:173
  921.6 5.4 fusion.132
  927.7 5.4 fusion.140
  933.1 6.1 add_bitcast_fusion
  939.6 33.7 %all-gather.21.cloned.1.call-done = bf16[512,2048]{1,0:T(8,128)(2,1)} async-done(((bf16[128,2048]{1,0:T(8,128)(2,1)}), bf16[512,2048]{1,0:T(8,128)(2,1)}) %all-gather.21.cloned.1.call-update) | async-done | bytes 2097168 | tf_op jit(solution)/shard_map/all_gather | solution.py:169
  973.3 3.0 convolution_convert_fusion.1
  976.4 5.0 fusion.8
  982.8 2.7 fusion.18
  988.8 31.1 %all-gather.25.cloned.1.call-done = bf16[512,2048]{1,0:T(8,128)(2,1)} async-done(((bf16[128,2048]{1,0:T(8,128)(2,1)}), bf16[512,2048]{1,0:T(8,128)(2,1)}) %all-gather.25.cloned.1.call-update) | async-done | bytes 2097168 | tf_op jit(solution)/shard_map/all_gather | solution.py:169
  1019.8 2.9 convolution_convert_fusion
  1022.8 5.1 fusion.4
  1029.9 2.7 fusion.19
  1037.0 4.1 convolution_bitcast_fusion.3
  1042.8 5.8 fusion.42
  1048.5 4.0 fusion.111
  1054.8 4.4 add_bitcast_fusion.1
  1059.2 5.6 fusion.25
  1065.1 5.7 fusion.27
  1075.7 13.4 fusion.21
  1092.1 16.8 %convolution_add_fusion = f32[2048,2,1408]{2,0,1:T(8,128)} fusion(f32[2048,2,1408]{2,0,1:T(8,128)} %fusion.21, bf16[512,2048,1]{1,0,2:T(8,128)(2,1)} %bitcast.50, bf16[512,2,1408]{0,2,1:T(8,128)(2,1)} %copy.110), kind=kOutput, calls=%fused_computation | convolution fusion | flops 5911347200 | bytes 51118080 | tf_op jit(solution)/shard_map/dot_general | solution.py:153
  1110.0 2.9 fusion.139
  1113.0 3.4 convolution_add_fusion.1
  1119.8 3.2 copy.114
  1123.0 45.6 %reduce-scatter.29.cloned.1.call-done = f32[256,1,640]{2,0,1:T(8,128)} async-done(((f32[2048,1,640]{2,0,1:T(8,128)}), f32[256,1,640]{2,0,1:T(8,128)}) %reduce-scatter.29.cloned.1.call-update) | async-done | bytes 655376 | tf_op jit(solution)/shard_map/reduce_scatter | solution.py:296
  1171.2 76.4 %reduce-scatter.27.cloned.1.call-done = f32[128,2048]{1,0:T(8,128)} async-done(((f32[512,2048]{1,0:T(8,128)}), f32[128,2048]{1,0:T(8,128)}) %reduce-scatter.27.cloned.1.call-update) | async-done | bytes 1048592 | tf_op jit(solution)/shard_map/reduce_scatter | solution.py:182
  1247.6 79.5 %reduce-scatter.23.cloned.1.call-done = f32[128,2048]{1,0:T(8,128)} async-done(((f32[512,2048]{1,0:T(8,128)}), f32[128,2048]{1,0:T(8,128)}) %reduce-scatter.23.cloned.1.call-update) | async-done | bytes 1048592 | tf_op jit(solution)/shard_map/reduce_scatter | solution.py:182
  1329.2 23.7 %all-reduce.2 = (f32[2048]{0:T(1024)S(1)}, f32[2048]{0:T(1024)S(1)}) all-reduce(f32[2048]{0:T(1024)S(1)} %add.202, f32[2048]{0:T(1024)S(1)} %add.206), channel_id=10, replica_groups=mesh['dp'=8,'tensor'=4] {'dp'}, use_global_device_ids=true, to_apply=%region_26.27.clone | all-reduce | flops 4096 | bytes 32768
  1353.0 12.0 all-reduce.3
  1368.9 108.7 %reduce-scatter.33.cloned.1.call-done = f32[256,2,1408]{2,0,1:T(8,128)} async-done(((f32[2048,2,1408]{2,0,1:T(8,128)}), f32[256,2,1408]{2,0,1:T(8,128)}) %reduce-scatter.33.cloned.1.call-update) | async-done | bytes 2883600 | tf_op jit(solution)/shard_map/reduce_scatter | solution.py:296
  1477.6 5.6 copy.113
  1483.2 49.4 %reduce-scatter.31.cloned.1.call-done = f32[256,512]{1,0:T(8,128)} async-done(((f32[2048,512]{1,0:T(8,128)}), f32[256,512]{1,0:T(8,128)}) %reduce-scatter.31.cloned.1.call-update) | async-done | bytes 524304 | tf_op jit(solution)/shard_map/reduce_scatter | solution.py:296
  (300 shorter events, 87.2 us)
Async XLA Ops:
  7.2 14.2 copy-start.2
  7.2 77.2 %all-gather.11.cloned.1.call-start = ((), (), s32[]{:S(2)}) async-start(), calls=%async_computation.16 | async-start | bytes 2949120 | tf_op jit(solution)/shard_map/all_gather | solution.py:209
  75.6 6.9 copy-start.79
  77.2 52.4 %all-to-all-start = ((bf16[4,128,2048]{2,1,0:T(8,128)(2,1)}), bf16[4,128,2048]{2,1,0:T(8,128)(2,1)}, u32[]{:S(2)}, u32[]{:S(2)}) async-start(bf16[4,128,2048]{2,1,0:T(8,128)(2,1)} %stack.69), calls=%async_computation | async-start | bytes 4194304 | tf_op jit(solution)/shard_map/all_to_all | solution.py:16
  81.7 62.7 %all-gather.13.cloned.1.call-start = ((), (), s32[]{:S(2)}) async-start(), calls=%async_computation.17 | async-start | bytes 2359296 | tf_op jit(solution)/shard_map/all_gather | solution.py:210
  82.4 142.1 %reduce-scatter.17.cloned.1.call-start = ((), (), s32[]{:S(2)}) async-start(), calls=%async_computation.22 | async-start | bytes 5242880 | tf_op jit(solution)/shard_map/reduce_scatter | solution.py:173
  82.9 51.0 %copy-start.68 = (f32[512]{0:T(512)}, f32[512]{0:T(512)S(1)}, u32[]{:S(2)}) copy-start(f32[512]{0:T(512)S(1)} %get-tuple-element.119) | copy-start | bytes 6148
  82.9 51.0 %copy-start.70 = (f32[512]{0:T(512)}, f32[512]{0:T(512)S(1)}, u32[]{:S(2)}) copy-start(f32[512]{0:T(512)S(1)} %get-tuple-element.120) | copy-start | bytes 6148
  83.1 57.4 %copy-start.13 = (pred[512,512]{0,1:T(8,128)(4,1)}, pred[512,512]{0,1:T(8,128)(4,1)S(1)}, u32[]{:S(2)}) copy-start(pred[512,512]{0,1:T(8,128)(4,1)S(1)} %fusion.59) | copy-start | bytes 786436
  83.1 50.8 %copy-start.77 = (f32[32]{0:T(128)}, f32[32]{0:T(128)S(1)}, u32[]{:S(2)}) copy-start(f32[32]{0:T(128)S(1)} %multiply_exponential_fusion) | copy-start | bytes 388
  129.6 7.4 copy-start.19
  129.6 7.4 copy-start.54
  129.6 7.4 copy-start.56
  137.0 16.3 %copy-start.51 = (bf16[512,32]{1,0:T(8,128)(2,1)}, bf16[512,32]{1,0:T(8,128)(2,1)S(1)}, u32[]{:S(2)}) copy-start(bf16[512,32]{1,0:T(8,128)(2,1)S(1)} %get-tuple-element.70) | copy-start | bytes 98308
  144.3 5.1 copy-start.24
  149.4 154.6 %reduce-scatter.13.cloned.1.call-start = ((), (), s32[]{:S(2)}) async-start(), calls=%async_computation.18 | async-start | bytes 5242880 | tf_op jit(solution)/shard_map/reduce_scatter | solution.py:173
  164.8 209.6 %all-gather.15.cloned.1.call-start = ((), (), s32[]{:S(2)}) async-start(), calls=%async_computation.19 | async-start | bytes 12976128 | tf_op jit(solution)/shard_map/all_gather | solution.py:212
  167.5 254.6 %all-gather.19.cloned.1.call-start = ((), (), s32[]{:S(2)}) async-start(), calls=%async_computation.24 | async-start | bytes 2621440 | tf_op jit(solution)/shard_map/all_gather | solution.py:169
  170.3 295.7 %all-gather.17.cloned.1.call-start = ((), (), s32[]{:S(2)}) async-start(), calls=%async_computation.20 | async-start | bytes 6488064 | tf_op jit(solution)/shard_map/all_gather | solution.py:213
  308.5 81.1 %all-to-all-start.1 = ((bf16[4,128,2048]{2,1,0:T(8,128)(2,1)}), bf16[4,128,2048]{2,1,0:T(8,128)(2,1)S(1)}, u32[]{:S(2)}, u32[]{:S(2)}) async-start(bf16[4,128,2048]{2,1,0:T(8,128)(2,1)} %stack.70), calls=%async_computation.2 | async-start | bytes 4194304 | tf_op jit(solution)/shard_map/all_to_all | solution.py:16
  312.7 251.2 %reduce-scatter.21.cloned.1.call-start = ((), (), s32[]{:S(2)}) async-start(), calls=%async_computation.25 | async-start | bytes 5242880 | tf_op jit(solution)/shard_map/reduce_scatter | solution.py:182
  389.6 11.9 copy-start.39
  487.0 77.0 %copy-start.7 = (f32[128,2048]{1,0:T(8,128)S(1)}, f32[128,2048]{1,0:T(8,128)}, u32[]{:S(2)}) copy-start(f32[128,2048]{1,0:T(8,128)} %get-tuple-element.69) | copy-start | bytes 3145732
  567.7 87.0 %all-to-all-start.3 = ((bf16[4,128,2048]{2,1,0:T(8,128)(2,1)}), bf16[4,128,2048]{2,1,0:T(8,128)(2,1)}, u32[]{:S(2)}, u32[]{:S(2)}) async-start(bf16[4,128,2048]{2,1,0:T(8,128)(2,1)} %stack.74), calls=%async_computation.6 | async-start | bytes 4194304 | tf_op jit(solution)/shard_map/all_to_all | solution.py:16
  572.2 94.3 %all-gather.23.cloned.1.call-start = ((), (), s32[]{:S(2)}) async-start(), calls=%async_computation.28 | async-start | bytes 2621440 | tf_op jit(solution)/shard_map/all_gather | solution.py:169
  572.9 189.6 %reduce-scatter.25.cloned.1.call-start = ((), (), s32[]{:S(2)}) async-start(), calls=%async_computation.29 | async-start | bytes 5242880 | tf_op jit(solution)/shard_map/reduce_scatter | solution.py:182
  687.4 154.7 %reduce-scatter.15.cloned.1.call-start = ((), (), s32[]{:S(2)}) async-start(), calls=%async_computation.21 | async-start | bytes 5242880 | tf_op jit(solution)/shard_map/reduce_scatter | solution.py:173
  699.9 221.7 %reduce-scatter.19.cloned.1.call-start = ((), (), s32[]{:S(2)}) async-start(), calls=%async_computation.23 | async-start | bytes 5242880 | tf_op jit(solution)/shard_map/reduce_scatter | solution.py:173
  712.5 209.1 %copy-start.20 = (f32[128,2048]{1,0:T(8,128)S(1)}, f32[128,2048]{1,0:T(8,128)}, u32[]{:S(2)}) copy-start(f32[128,2048]{1,0:T(8,128)} %reduce-scatter.21.cloned.1.call-done) | copy-start | bytes 3145732
  712.6 260.8 %all-gather.21.cloned.1.call-start = ((), (), s32[]{:S(2)}) async-start(), calls=%async_computation.26 | async-start | bytes 2621440 | tf_op jit(solution)/shard_map/all_gather | solution.py:169
  927.0 92.8 %all-gather.25.cloned.1.call-start = ((), (), s32[]{:S(2)}) async-start(), calls=%async_computation.30 | async-start | bytes 2621440 | tf_op jit(solution)/shard_map/all_gather | solution.py:169
  927.6 5.5 copy-start.10
  927.6 192.2 %reduce-scatter.35.cloned.1.call-start = ((), (), s32[]{:S(2)}) async-start(), calls=%async_computation.35 | async-start | bytes 12976128 | tf_op jit(solution)/shard_map/reduce_scatter | solution.py:296
  927.6 5.4 copy-start.38
  939.1 34.2 %copy-start.12 = (bf16[2048,512]{1,0:T(8,128)(2,1)S(1)}, bf16[2048,512]{1,0:T(8,128)(2,1)}, u32[]{:S(2)}) copy-start(bf16[2048,512]{1,0:T(8,128)(2,1)} %all-gather.13.cloned.1.call-done) | copy-start | bytes 6291460
  939.1 229.5 %reduce-scatter.29.cloned.1.call-start = ((), (), s32[]{:S(2)}) async-start(), calls=%async_computation.32 | async-start | bytes 5898240 | tf_op jit(solution)/shard_map/reduce_scatter | solution.py:296
  976.3 5.1 copy-start.60
  976.4 5.1 slice-start.4
  976.4 6.4 slice-start.5
  982.8 4.7 copy-start.35
  982.8 4.7 copy-start.37
  988.8 34.0 %copy-start.14 = (pred[512,512]{0,1:T(8,128)(4,1)S(1)}, pred[512,512]{0,1:T(8,128)(4,1)}, u32[]{:S(2)}) copy-start(pred[512,512]{0,1:T(8,128)(4,1)} %copy-done.13) | copy-start | bytes 786436
  988.8 34.0 %copy-start.65 = (f32[8,512]{1,0:T(8,128)S(1)}, f32[8,512]{1,0:T(8,128)}, u32[]{:S(2)}) copy-start(f32[8,512]{1,0:T(8,128)} %copy-done.64) | copy-start | bytes 49156
  1022.7 5.2 copy-start.62
  1022.7 5.2 slice-start
  1022.8 7.1 slice-start.1
  1036.9 4.6 copy-start.6
  1037.0 4.6 copy-start.48
  1037.0 4.6 copy-start.50
  1041.6 11.0 slice-start.2
  1042.8 9.8 slice-start.3
  1059.2 188.4 %reduce-scatter.27.cloned.1.call-start = ((), (), s32[]{:S(2)}) async-start(), calls=%async_computation.31 | async-start | bytes 5242880 | tf_op jit(solution)/shard_map/reduce_scatter | solution.py:182
  1064.8 262.3 %reduce-scatter.23.cloned.1.call-start = ((), (), s32[]{:S(2)}) async-start(), calls=%async_computation.27 | async-start | bytes 5242880 | tf_op jit(solution)/shard_map/reduce_scatter | solution.py:182
  1070.8 406.8 %reduce-scatter.33.cloned.1.call-start = ((), (), s32[]{:S(2)}) async-start(), calls=%async_computation.34 | async-start | bytes 25952256 | tf_op jit(solution)/shard_map/reduce_scatter | solution.py:296
  1075.7 13.4 copy-start.44
  1075.7 13.4 copy-start.46
  1109.0 423.6 %reduce-scatter.31.cloned.1.call-start = ((), (), s32[]{:S(2)}) async-start(), calls=%async_computation.33 | async-start | bytes 4718592 | tf_op jit(solution)/shard_map/reduce_scatter | solution.py:296
  1119.8 207.3 %copy-start.3 = (f32[2,128,2048]{2,1,0:T(8,128)S(1)}, f32[2,128,2048]{2,1,0:T(8,128)}, u32[]{:S(2)}) copy-start(f32[2,128,2048]{2,1,0:T(8,128)} %param.9) | copy-start | bytes 6291460
  1119.8 207.3 %copy-start.67 = (f32[8,1,256]{2,1,0:T(1,128)S(1)}, f32[8,1,256]{2,1,0:T(1,128)}, u32[]{:S(2)}) copy-start(f32[8,1,256]{2,1,0:T(1,128)} %copy-done.66) | copy-start | bytes 24580
  1119.8 207.3 %copy-start.74 = (f32[128]{0:T(128)S(1)}, f32[128]{0:T(128)}, u32[]{:S(2)}) copy-start(f32[128]{0:T(128)} %copy-done.73) | copy-start | bytes 1540
  1119.8 207.3 %copy-start.76 = (f32[128]{0:T(128)S(1)}, f32[128]{0:T(128)}, u32[]{:S(2)}) copy-start(f32[128]{0:T(128)} %copy-done.75) | copy-start | bytes 1540
  1123.0 242.0 %copy-start.80 = (f32[128]{0:T(128)S(1)}, f32[128]{0:T(128)}, u32[]{:S(2)}) copy-start(f32[128]{0:T(128)} %get-tuple-element.97) | copy-start | bytes 1540
  1123.0 242.0 %copy-start.81 = (f32[128]{0:T(128)S(1)}, f32[128]{0:T(128)}, u32[]{:S(2)}) copy-start(f32[128]{0:T(128)} %get-tuple-element.118) | copy-start | bytes 1540
  1247.6 117.4 %copy-start.23 = (f32[128,2048]{1,0:T(8,128)S(1)}, f32[128,2048]{1,0:T(8,128)}, u32[]{:S(2)}) copy-start(f32[128,2048]{1,0:T(8,128)} %reduce-scatter.27.cloned.1.call-done) | copy-start | bytes 3145732
  (50 other events, 112.6 us)
Sparse Core Ops, SparseCore 0:
  9.9 32.6 all-gather.10
  84.4 28.2 all-gather.12
  149.5 74.9 reduce-scatter.16
  226.7 77.2 reduce-scatter.12
  306.3 68.0 all-gather.14
  376.4 45.6 all-gather.18
  424.0 41.9 all-gather.16
  487.1 76.7 reduce-scatter.20
  575.1 74.1 all-gather.22
  687.5 74.9 reduce-scatter.24
  764.8 77.2 reduce-scatter.14
  844.2 77.2 reduce-scatter.18
  927.1 46.1 all-gather.20
  975.3 44.4 all-gather.24
  1023.2 85.6 reduce-scatter.34
  1112.1 56.4 reduce-scatter.28
  1170.8 76.7 reduce-scatter.26
  1249.8 77.2 reduce-scatter.22
  1330.7 146.8 reduce-scatter.32
  1481.4 51.1 reduce-scatter.30
